TPU v7x, 32 devices: a whole 2x2x4 slice. The times are simulated.
32 devices in a mesh: occ: 2 (over x), vir: 4 (over z), aux: 4 (over y, core).
Axes of the slice: x: 2, y: 2, z: 4, core: 2. Of those that a mesh axis runs over, the one named last changes fastest.
Arguments:
- amplitudes: bfloat16 [16, 1024, 1024], P('occ', 'vir'), may hold values from -6 to 6
- pair_mask: int32 [16, 8, 8], P('occ', 'vir'), may hold values 0 or 1
- left_factor: bfloat16 [32, 1024, 4096], P(None, 'vir', 'aux'), may hold values from -0.0390625 to 0.0390625
- left_mask: int32 [8, 32], P('vir', 'aux'), may hold values 0 or 1
- right_factor: bfloat16 [1024, 4, 4096], P(('occ', 'vir'), None, 'aux'), may hold values from -0.0390625 to 0.0390625
- right_mask: int32 [8, 32], P(None, 'aux'), may hold values 0 or 1
- residual_in: float32 [16, 4, 32], P('occ'), may hold values from -6 to 6
Outputs:
- updated: float32 [16, 4, 32], P('occ')
All inputs are finite; a program needn't handle non-finite values. No bound on the sum of `pair_mask` or of `left_mask` or of `right_mask` on one device may be relied on, other than what follows from the above.
Results may differ from a plain program's by a relative error of at most 0.0003.
Values may be sent and summed in bfloat16 or wider, within the bound.
No kernel may reach another device: no remote copies, remote signals or barrier semaphores. Data moves between devices by JAX's collectives and lax.ppermute only.
A program may use at most 128 MiB of HBM per device.

v0:
```python
import jax
import jax.numpy as jnp
from jax import lax
from jax.sharding import PartitionSpec as P

TILE = 128


def expand_tiles(mask, width):
    return jnp.repeat(jnp.repeat(mask, width, axis=-2), width, axis=-1)


def local(amplitudes, pair_mask, left_factor, left_mask, right_factor, right_mask, residual_in):
    pairs_here, cols_here, virt_all = amplitudes.shape
    rows_here, block_b, aux_here = right_factor.shape
    tau = amplitudes * expand_tiles(pair_mask, TILE).astype(jnp.bfloat16)
    left = left_factor * expand_tiles(left_mask, TILE).astype(jnp.bfloat16)[None, :, :]
    tiles_all = right_mask.shape[0]
    aux_mask = jnp.repeat(right_mask, TILE, axis=1).astype(jnp.float32)
    row_start = lax.axis_index(("occ", "vir")) * rows_here
    row_tiles = (row_start + jnp.arange(rows_here, dtype=jnp.int32)) // TILE
    onehot = (row_tiles[:, None] == jnp.arange(tiles_all, dtype=jnp.int32)[None, :]).astype(
        jnp.float32
    )
    row_mask = jnp.dot(onehot, aux_mask, preferred_element_type=jnp.float32)
    right = right_factor * row_mask.astype(jnp.bfloat16)[:, None, :]
    right_whole = lax.all_gather(right, ("occ", "vir"), axis=0, tiled=True)
    tau_flat = tau.reshape(pairs_here * cols_here, virt_all)
    left_wide = left.astype(jnp.float32)
    columns = []
    for index_b in range(block_b):
        inner_b = jnp.dot(tau_flat, right_whole[:, index_b, :], preferred_element_type=jnp.float32)
        inner_b = inner_b.reshape(pairs_here, cols_here, aux_here)
        columns.append(
            jnp.einsum(
                "pcq,acq->pa",
                inner_b,
                left_wide,
                precision=lax.Precision.HIGHEST,
                preferred_element_type=jnp.float32,
            )
        )
    partial_sum = jnp.stack(columns, axis=1)
    total = lax.psum(partial_sum, ("vir", "aux"))
    return residual_in + total


def solution(mesh):
    return jax.shard_map(
        local,
        mesh=mesh,
        in_specs=(
            P("occ", "vir", None),
            P("occ", "vir", None),
            P(None, "vir", "aux"),
            P("vir", "aux"),
            P(("occ", "vir"), None, "aux"),
            P(None, "aux"),
            P("occ", None, None),
        ),
        out_specs=P("occ", None, None),
        check_vma=False,
    )
```

profile of v0, /device:TPU:0, one launch (start us, length us, event | category | flops | bytes accessed | tf_op | source)
XLA Modules:
  0.0 383.0 jit_solution(14707230647622306978)
XLA Ops:
  6.5 0.7 convert_element_type.41
  7.2 0.1 broadcast_bitcast_fusion
  7.3 0.3 convolution_convert_fusion
  7.6 3.0 copy_multiply_fusion
  10.6 0.0 all-gather.2.cloned.1.call-update
  10.6 0.7 convert_element_type.38
  11.3 0.1 broadcast_in_dim.19
  11.4 3.8 %broadcast_in_dim.20 = bf16[8,256,8,128]{3,2,1,0:T(8,128)(2,1)} broadcast(bf16[8,256,8]{2,1,0:T(8,128)(2,1)S(1)} %bitcast.46), dimensions={0,1,2} | broadcast | bytes 4227072 | tf_op jit(solution)/shard_map/broadcast_in_dim | solution.py:10
  15.2 7.4 %convert_element_type.40 = bf16[8,256,1024]{2,1,0:T(8,128)(2,1)} reshape(bf16[8,256,8,128]{3,2,1,0:T(8,128)(2,1)} %broadcast_in_dim.20) | data formatting | bytes 8388608 | tf_op jit(solution)/shard_map/convert_element_type | solution.py:16
  22.7 0.3 broadcast_in_dim.23
  23.0 0.1 copy.55
  23.1 7.9 %mul.25 = bf16[8,256,1024]{2,1,0:T(8,128)(2,1)} multiply(bf16[8,256,1024]{2,1,0:T(8,128)(2,1)} %param.7, bf16[8,256,1024]{2,1,0:T(8,128)(2,1)} %convert_element_type.40) | non-fusion elementwise | flops 2097152 | bytes 12582912 | tf_op jit(solution)/shard_map/mul | solution.py:16
  31.0 13.8 %broadcast_multiply_fusion = bf16[32,256,1024]{2,1,0:T(8,128)(2,1)} fusion(bf16[32,256,1024]{2,1,0:T(8,128)(2,1)} %param.9, bf16[256,1024]{1,0:T(8,128)(2,1)S(1)} %bitcast.45), kind=kLoop, calls=%fused_computation.8 | loop fusion | flops 8388608 | bytes 34078720 | tf_op jit(solution)/shard_map/mul | solution.py:17
  44.9 93.1 %all-gather.2.cloned.1.call-done = bf16[1024,4,1024]{2,0,1:T(8,128)(2,1)} async-done(((bf16[128,4,1024]{2,0,1:T(8,128)(2,1)}), bf16[1024,4,1024]{2,0,1:T(8,128)(2,1)}) %all-gather.2.cloned.1.call-update) | async-done | bytes 8388624 | tf_op jit(solution)/shard_map/all_gather | solution.py:27
  138.0 11.6 %fusion.14 = f32[8,256,1024]{2,0,1:T(8,128)} fusion(bf16[8,256,1024]{2,1,0:T(8,128)(2,1)} %mul.25, bf16[1024,4,1024]{2,0,1:T(8,128)(2,1)} %all-gather.2.cloned.1.call-done), kind=kOutput, calls=%fused_computation.15 | convolution fusion | flops 4294967296 | bytes 14680064 | tf_op jit(solution)/shard_map/dot_general | solution.py:32
  149.6 32.4 %fusion.16 = f32[8,1,32]{2,0,1:T(8,128)S(1)} fusion(f32[8,256,1024]{2,0,1:T(8,128)} %fusion.14, bf16[32,256,1024]{2,1,0:T(8,128)(2,1)S(1)} %copy-done), kind=kOutput, calls=%fused_computation.22 | convolution fusion | flops 805306368 | bytes 25166848 | tf_op jit(solution)/shard_map/pcq,acq->pa/dot_general | solution.py:35
  181.9 12.3 %fusion.12 = f32[8,256,1024]{2,0,1:T(8,128)} fusion(bf16[8,256,1024]{2,1,0:T(8,128)(2,1)S(1)} %copy-done.1, bf16[1024,4,1024]{2,0,1:T(8,128)(2,1)} %all-gather.2.cloned.1.call-done), kind=kOutput, calls=%fused_computation.13 | convolution fusion | flops 4294967296 | bytes 14680064 | tf_op jit(solution)/shard_map/dot_general | solution.py:32
  194.2 32.6 %fusion.19 = f32[8,1,32]{2,0,1:T(8,128)S(1)} fusion(f32[8,256,1024]{2,0,1:T(8,128)} %fusion.12, bf16[32,256,1024]{2,1,0:T(8,128)(2,1)S(1)} %copy-done), kind=kOutput, calls=%fused_computation.23 | convolution fusion | flops 805306368 | bytes 25166848 | tf_op jit(solution)/shard_map/pcq,acq->pa/dot_general | solution.py:35
  226.8 12.3 %fusion.10 = f32[8,256,1024]{2,0,1:T(8,128)} fusion(bf16[8,256,1024]{2,1,0:T(8,128)(2,1)S(1)} %copy-done.1, bf16[1024,4,1024]{2,0,1:T(8,128)(2,1)} %all-gather.2.cloned.1.call-done), kind=kOutput, calls=%fused_computation.11 | convolution fusion | flops 4294967296 | bytes 14680064 | tf_op jit(solution)/shard_map/dot_general | solution.py:32
  239.1 32.4 %fusion.22 = f32[8,1,32]{2,0,1:T(8,128)S(1)} fusion(f32[8,256,1024]{2,0,1:T(8,128)} %fusion.10, bf16[32,256,1024]{2,1,0:T(8,128)(2,1)S(1)} %copy-done), kind=kOutput, calls=%fused_computation.24 | convolution fusion | flops 805306368 | bytes 25166848 | tf_op jit(solution)/shard_map/pcq,acq->pa/dot_general | solution.py:35
  271.5 12.3 %fusion.8 = f32[8,256,1024]{2,0,1:T(8,128)} fusion(bf16[8,256,1024]{2,1,0:T(8,128)(2,1)S(1)} %copy-done.1, bf16[1024,4,1024]{2,0,1:T(8,128)(2,1)} %all-gather.2.cloned.1.call-done), kind=kOutput, calls=%fused_computation.9 | convolution fusion | flops 4294967296 | bytes 14680064 | tf_op jit(solution)/shard_map/dot_general | solution.py:32
  283.8 32.2 %fusion.25 = f32[8,1,32]{2,0,1:T(8,128)S(1)} fusion(f32[8,256,1024]{2,0,1:T(8,128)} %fusion.8, bf16[32,256,1024]{2,1,0:T(8,128)(2,1)S(1)} %copy-done), kind=kOutput, calls=%fused_computation.25 | convolution fusion | flops 805306368 | bytes 25166848 | tf_op jit(solution)/shard_map/pcq,acq->pa/dot_general | solution.py:35
  316.0 59.4 %psum.7 = f32[8,4,32]{2,0,1:T(8,128)S(1)} all-reduce(f32[8,4,32]{2,0,1:T(8,128)S(1)} %pad_maximum_fusion), channel_id=1, replica_groups=mesh['occ'=2,'vir'=4,'aux'=4] {'vir','aux'}, use_global_device_ids=true, to_apply=%region_0.1 | all-reduce | flops 1024 | bytes 8192 | tf_op jit(solution)/shard_map/psum | solution.py:44
  375.4 0.6 copy.20
  (14 shorter events, 0.1 us)
Async XLA Ops:
  6.5 131.4 %all-gather.2.cloned.1.call-start = ((), (), s32[]{:S(2)}) async-start(), calls=%async_computation | async-start | bytes 9437184 | tf_op jit(solution)/shard_map/all_gather | solution.py:27
  7.6 15.1 %copy-start.3 = (s32[2,8]{1,0:T(2,128)S(1)}, s32[2,8]{1,0:T(2,128)}, u32[]{:S(2)}) copy-start(s32[2,8]{1,0:T(2,128)} %param.10) | copy-start | bytes 196
  138.0 11.6 %copy-start = (bf16[32,256,1024]{2,1,0:T(8,128)(2,1)S(1)}, bf16[32,256,1024]{2,1,0:T(8,128)(2,1)}, u32[]{:S(2)}) copy-start(bf16[32,256,1024]{2,1,0:T(8,128)(2,1)} %broadcast_multiply_fusion) | copy-start | bytes 50331652
  149.6 32.4 %copy-start.1 = (bf16[8,256,1024]{2,1,0:T(8,128)(2,1)S(1)}, bf16[8,256,1024]{2,1,0:T(8,128)(2,1)}, u32[]{:S(2)}) copy-start(bf16[8,256,1024]{2,1,0:T(8,128)(2,1)} %mul.25) | copy-start | bytes 12582916
  283.8 91.6 %copy-start.2 = (f32[8,4,32]{2,1,0:T(4,128)S(1)}, f32[8,4,32]{2,1,0:T(4,128)}, u32[]{:S(2)}) copy-start(f32[8,4,32]{2,1,0:T(4,128)} %param.13) | copy-start | bytes 12292
Sparse Core Ops, SparseCore 0:
  10.7 127.1 all-gather.1
where the time goes:
time: 391 us; the launch traced here: 383 us
  matrix products  178 us (46%)
  waiting for transfers between devices  93.1 us (24%)
  blocking collectives  59.4 us (15%)
  other arithmetic  26.2 us (7%)
  between operations  13.6 us (3%)
  local copies, waits for them, and re-layouts  12.5 us (3%)
    dot_general x4, matrix products, local(): jnp.einsum('pcq,acq->pa', inner_b, left_wide, precision=lax.Precision.HIG...  130 us
    all_gather x1, waiting for transfers between devices, local(): right_whole = lax.all_gather(right, ('occ', 'vir'), axis=0, tiled=True)  93.1 us
    psum x1, blocking collectives, local(): total = lax.psum(partial_sum, ('vir', 'aux'))  59.4 us
    dot_general x4, matrix products, local(): jnp.dot(tau_flat, right_whole[:, index_b, :], preferred_element_type=jnp....  48.4 us
    mul x1, other arithmetic, local(): left_factor * expand_tiles(left_mask, TILE).astype(jnp.bfloat16)[None, :, :]  13.8 us
    mul x1, other arithmetic, local(): tau = amplitudes * expand_tiles(pair_mask, TILE).astype(jnp.bfloat16)  7.92 us
  transfers between devices with their start and end apart: 1, of which 1 were waited for; matrix products, arithmetic and copies ran while one was open for 9% of the time, Pallas kernels for 0%

commit v1 on v0

--- a/solution.py
+++ b/solution.py
@@ -4,6 +4,18 @@
 from jax.sharding import PartitionSpec as P
 
 TILE = 128
+
+
+def form_the_terms(local_array):
+    return jnp.concatenate(
+        lax.all_to_all(
+            jnp.stack([local_array] * lax.axis_size(("occ", "vir"))),
+            axis_name=("occ", "vir"),
+            split_axis=0,
+            concat_axis=0,
+        ),
+        axis=0,
+    )
 
 
 def expand_tiles(mask, width):
@@ -24,7 +36,7 @@
     )
     row_mask = jnp.dot(onehot, aux_mask, preferred_element_type=jnp.float32)
     right = right_factor * row_mask.astype(jnp.bfloat16)[:, None, :]
-    right_whole = lax.all_gather(right, ("occ", "vir"), axis=0, tiled=True)
+    right_whole = form_the_terms(right)
     tau_flat = tau.reshape(pairs_here * cols_here, virt_all)
     left_wide = left.astype(jnp.float32)
     columns = []

time: 391 us -> 459 us (1.17)
  waiting for transfers between devices: 93.1 us -> 151 us
  between operations: 13.6 us -> 0.49 us
  local copies, waits for them, and re-layouts: 12.5 us -> 25.3 us
  starting transfers between devices: 0.01 us -> 7.42 us
  matrix products: 178 us -> 185 us
    all_to_all x0 -> x1, waiting for transfers between devices: none -> 151 us  [form_the_terms(): lax.all_to_all(jnp.stack([local_array] * lax.axis_size(('occ', 'vir'))),...]
    all_gather x1 -> x0, waiting for transfers between devices: 93.1 us -> none  [local(): right_whole = lax.all_gather(right, ('occ', 'vir'), axis=0, tiled=True)]
    dot_general x4, matrix products: 130 us -> 139 us  [local(): jnp.einsum('pcq,acq->pa', inner_b, left_wide, precision=lax.Precision.HIG...]
    all_to_all x0 -> x1, local copies, waits for them, and re-layouts: none -> 8.34 us  [form_the_terms(): lax.all_to_all(jnp.stack([local_array] * lax.axis_size(('occ', 'vir'))),...]
    all_to_all x0 -> x1, starting transfers between devices: none -> 7.42 us  [form_the_terms(): lax.all_to_all(jnp.stack([local_array] * lax.axis_size(('occ', 'vir'))),...]
  transfers between devices with their start and end apart: 1 -> 1, of which waited for: 1 -> 1; matrix products, arithmetic and copies ran while one was open for 9% -> 7% of each run, Pallas kernels for 0% -> 0%
where the time goes in v1:
time: 459 us; the launch traced here: 451 us
  matrix products  185 us (40%)
  waiting for transfers between devices  151 us (33%)
  blocking collectives  57.6 us (13%)
  local copies, waits for them, and re-layouts  25.3 us (6%)
  other arithmetic  24.2 us (5%)
  starting transfers between devices  7.42 us (2%)
    all_to_all x1, waiting for transfers between devices, form_the_terms(): lax.all_to_all(jnp.stack([local_array] * lax.axis_size(('occ', 'vir'))),...  151 us
    dot_general x4, matrix products, local(): jnp.einsum('pcq,acq->pa', inner_b, left_wide, precision=lax.Precision.HIG...  139 us
    psum x1, blocking collectives, local(): total = lax.psum(partial_sum, ('vir', 'aux'))  57.6 us
    dot_general x4, matrix products, local(): jnp.dot(tau_flat, right_whole[:, index_b, :], preferred_element_type=jnp....  45.9 us
    mul x1, other arithmetic, local(): left_factor * expand_tiles(left_mask, TILE).astype(jnp.bfloat16)[None, :, :]  13.8 us
  transfers between devices with their start and end apart: 1, of which 1 were waited for; matrix products, arithmetic and copies ran while one was open for 7% of the time, Pallas kernels for 0%

profile of v1, /device:TPU:0, one launch (start us, length us, event | category | flops | bytes accessed | tf_op | source)
XLA Modules:
  0.0 451.0 jit_solution(1037591159827580294)
XLA Ops:
  0.0 0.7 convert_element_type.41
  0.8 0.3 convolution_convert_fusion
  1.1 1.8 broadcast_multiply_fusion.1
  2.9 0.3 copy.21
  3.2 4.3 stack.12
  7.5 7.4 %all-to-all-start = ((bf16[8,128,4,1024]{3,1,2,0:T(8,128)(2,1)}), bf16[8,128,4,1024]{3,1,2,0:T(8,128)(2,1)}, u32[]{:S(2)}, u32[]{:S(2)}) async-start(bf16[8,128,4,1024]{3,1,2,0:T(8,128)(2,1)} %stack.12), calls=%async_computation | async-start | bytes 16777216 | tf_op jit(solution)/shard_map/all_to_all | solution.py:11
  15.0 3.8 broadcast_in_dim.20
  18.9 7.3 %convert_element_type.40 = bf16[8,256,1024]{2,1,0:T(8,128)(2,1)} reshape(bf16[8,256,8,128]{3,2,1,0:T(8,128)(2,1)} %broadcast_in_dim.20) | data formatting | bytes 8388608 | tf_op jit(solution)/shard_map/convert_element_type | solution.py:28
  26.2 0.3 broadcast_in_dim.23
  26.6 0.1 copy.65
  26.7 7.8 %mul.25 = bf16[8,256,1024]{2,1,0:T(8,128)(2,1)} multiply(bf16[8,256,1024]{2,1,0:T(8,128)(2,1)} %param.7, bf16[8,256,1024]{2,1,0:T(8,128)(2,1)} %convert_element_type.40) | non-fusion elementwise | flops 2097152 | bytes 12582912 | tf_op jit(solution)/shard_map/mul | solution.py:28
  34.5 13.8 %broadcast_multiply_fusion = bf16[32,256,1024]{2,1,0:T(8,128)(2,1)} fusion(bf16[32,256,1024]{2,1,0:T(8,128)(2,1)} %param.9, bf16[256,1024]{1,0:T(8,128)(2,1)S(1)} %bitcast.52), kind=kLoop, calls=%fused_computation.8 | loop fusion | flops 8388608 | bytes 34078720 | tf_op jit(solution)/shard_map/mul | solution.py:29
  48.3 150.7 %all-to-all-done = bf16[8,128,4,1024]{3,1,2,0:T(8,128)(2,1)} async-done(((bf16[8,128,4,1024]{3,1,2,0:T(8,128)(2,1)}), bf16[8,128,4,1024]{3,1,2,0:T(8,128)(2,1)}, u32[]{:S(2)}, u32[]{:S(2)}) %all-to-all-start) | async-done | bytes 8388640 | tf_op jit(solution)/shard_map/all_to_all | solution.py:11
  199.0 8.3 %copy.22 = bf16[8,128,4,1024]{3,1,0,2:T(8,128)(2,1)} copy(bf16[8,128,4,1024]{3,1,2,0:T(8,128)(2,1)} %all-to-all-done) | data formatting | bytes 16777216 | tf_op jit(solution)/shard_map/all_to_all | solution.py:11
  207.3 12.3 %fusion.14 = f32[8,256,1024]{2,0,1:T(8,128)} fusion(bf16[8,256,1024]{2,1,0:T(8,128)(2,1)S(1)} %copy-done.1, bf16[1024,4,1024]{2,0,1:T(8,128)(2,1)} %bitcast.48), kind=kOutput, calls=%fused_computation.15 | convolution fusion | flops 4294967296 | bytes 14680064 | tf_op jit(solution)/shard_map/dot_general | solution.py:44
  219.6 10.8 %fusion.12 = f32[8,256,1024]{2,0,1:T(8,128)} fusion(bf16[8,256,1024]{2,1,0:T(8,128)(2,1)S(1)} %copy-done.1, bf16[1024,4,1024]{2,0,1:T(8,128)(2,1)S(1)} %bitcast.50), kind=kOutput, calls=%fused_computation.13 | convolution fusion | flops 4294967296 | bytes 14680064 | tf_op jit(solution)/shard_map/dot_general | solution.py:44
  230.4 10.6 %fusion.10 = f32[8,256,1024]{2,0,1:T(8,128)} fusion(bf16[8,256,1024]{2,1,0:T(8,128)(2,1)S(1)} %copy-done.1, bf16[1024,4,1024]{2,0,1:T(8,128)(2,1)S(1)} %bitcast.51), kind=kOutput, calls=%fused_computation.11 | convolution fusion | flops 4294967296 | bytes 14680064 | tf_op jit(solution)/shard_map/dot_general | solution.py:44
  241.0 12.2 %fusion.8 = f32[8,256,1024]{2,0,1:T(8,128)} fusion(bf16[8,256,1024]{2,1,0:T(8,128)(2,1)S(1)} %copy-done.1, bf16[1024,4,1024]{2,0,1:T(8,128)(2,1)} %bitcast.49), kind=kOutput, calls=%fused_computation.9 | convolution fusion | flops 4294967296 | bytes 14680064 | tf_op jit(solution)/shard_map/dot_general | solution.py:44
  253.2 42.1 %fusion.16 = f32[8,1,32]{2,0,1:T(8,128)S(1)} fusion(f32[8,256,1024]{2,0,1:T(8,128)} %fusion.14, bf16[32,256,1024]{2,1,0:T(8,128)(2,1)S(1)} %bitcast.47), kind=kOutput, calls=%fused_computation.22 | convolution fusion | flops 805306368 | bytes 25166848 | tf_op jit(solution)/shard_map/pcq,acq->pa/dot_general | solution.py:47
  295.4 32.5 %fusion.19 = f32[8,1,32]{2,0,1:T(8,128)S(1)} fusion(f32[8,256,1024]{2,0,1:T(8,128)} %fusion.12, bf16[32,256,1024]{2,1,0:T(8,128)(2,1)S(1)} %bitcast.47), kind=kOutput, calls=%fused_computation.23 | convolution fusion | flops 805306368 | bytes 25166848 | tf_op jit(solution)/shard_map/pcq,acq->pa/dot_general | solution.py:47
  327.8 32.2 %fusion.22 = f32[8,1,32]{2,0,1:T(8,128)S(1)} fusion(f32[8,256,1024]{2,0,1:T(8,128)} %fusion.10, bf16[32,256,1024]{2,1,0:T(8,128)(2,1)S(1)} %bitcast.47), kind=kOutput, calls=%fused_computation.24 | convolution fusion | flops 805306368 | bytes 25166848 | tf_op jit(solution)/shard_map/pcq,acq->pa/dot_general | solution.py:47
  360.0 32.3 %fusion.25 = f32[8,1,32]{2,0,1:T(8,128)S(1)} fusion(f32[8,256,1024]{2,0,1:T(8,128)} %fusion.8, bf16[32,256,1024]{2,1,0:T(8,128)(2,1)S(1)} %bitcast.47), kind=kOutput, calls=%fused_computation.25 | convolution fusion | flops 805306368 | bytes 25166848 | tf_op jit(solution)/shard_map/pcq,acq->pa/dot_general | solution.py:47
  392.3 57.6 %psum.7 = f32[8,4,32]{2,0,1:T(8,128)S(1)} all-reduce(f32[8,4,32]{2,0,1:T(8,128)S(1)} %pad_maximum_fusion), channel_id=1, replica_groups=mesh['occ'=2,'vir'=4,'aux'=4] {'vir','aux'}, use_global_device_ids=true, to_apply=%region_0.1 | all-reduce | flops 1024 | bytes 8192 | tf_op jit(solution)/shard_map/psum | solution.py:56
  450.0 0.6 copy.32
  (27 shorter events, 0.2 us)
Async XLA Ops:
  7.5 7.4 %copy-start.3 = (s32[8,2,8]{2,1,0:T(2,128)S(1)}, s32[8,2,8]{2,1,0:T(2,128)}, u32[]{:S(2)}) copy-start(s32[8,2,8]{2,1,0:T(2,128)} %param.8) | copy-start | bytes 1540
  7.5 191.4 %all-to-all-start = ((bf16[8,128,4,1024]{3,1,2,0:T(8,128)(2,1)}), bf16[8,128,4,1024]{3,1,2,0:T(8,128)(2,1)}, u32[]{:S(2)}, u32[]{:S(2)}) async-start(bf16[8,128,4,1024]{3,1,2,0:T(8,128)(2,1)} %stack.12), calls=%async_computation | async-start | bytes 16777216 | tf_op jit(solution)/shard_map/all_to_all | solution.py:11
  14.9 11.3 %copy-start.4 = (s32[2,8]{1,0:T(2,128)S(1)}, s32[2,8]{1,0:T(2,128)}, u32[]{:S(2)}) copy-start(s32[2,8]{1,0:T(2,128)} %param.10) | copy-start | bytes 196
  199.0 8.3 %copy-start.1 = (bf16[8,256,1024]{2,1,0:T(8,128)(2,1)S(1)}, bf16[8,256,1024]{2,1,0:T(8,128)(2,1)}, u32[]{:S(2)}) copy-start(bf16[8,256,1024]{2,1,0:T(8,128)(2,1)} %mul.25) | copy-start | bytes 12582916
  207.3 12.3 %copy-start = (bf16[8,128,4,1024]{3,1,0,2:T(8,128)(2,1)S(1)}, bf16[8,128,4,1024]{3,1,0,2:T(8,128)(2,1)}, u32[]{:S(2)}) copy-start(bf16[8,128,4,1024]{3,1,0,2:T(8,128)(2,1)} %copy.22) | copy-start | bytes 25165828
  230.4 22.8 %slice-start = ((s8[16777216]{0:T(1024)(128)(4,1)}), s8[4194304]{0:T(1024)(128)(4,1)S(1)}, s32[]{:S(2)}) async-start(s8[16777216]{0:T(1024)(128)(4,1)} %bitcast.46), calls=%async_computation.1 | async-start | bytes 8388608
  230.4 22.8 %slice-start.1 = ((s8[16777216]{0:T(1024)(128)(4,1)}), s8[4194304]{0:T(1024)(128)(4,1)S(1)}, s32[]{:S(2)}) async-start(s8[16777216]{0:T(1024)(128)(4,1)} %bitcast.46), calls=%async_computation.2 | async-start | bytes 8388608
  241.0 12.3 %slice-start.2 = ((s8[16777216]{0:T(1024)(128)(4,1)}), s8[4194304]{0:T(1024)(128)(4,1)S(1)}, s32[]{:S(2)}) async-start(s8[16777216]{0:T(1024)(128)(4,1)} %bitcast.46), calls=%async_computation.3 | async-start | bytes 8388608
  241.0 12.3 %slice-start.3 = ((s8[16777216]{0:T(1024)(128)(4,1)}), s8[4194304]{0:T(1024)(128)(4,1)S(1)}, s32[]{:S(2)}) async-start(s8[16777216]{0:T(1024)(128)(4,1)} %bitcast.46), calls=%async_computation.4 | async-start | bytes 8388608
  360.0 89.9 %copy-start.2 = (f32[8,4,32]{2,1,0:T(4,128)S(1)}, f32[8,4,32]{2,1,0:T(4,128)}, u32[]{:S(2)}) copy-start(f32[8,4,32]{2,1,0:T(4,128)} %param.13) | copy-start | bytes 12292
